TPU v7x, 32 devices: a whole 2x2x4 slice. The times are simulated.
32 devices in a mesh: ctx: 4 (over y, x), tp: 8 (over z, core).
Axes of the slice: x: 2, y: 2, z: 4, core: 2. Of those that a mesh axis runs over, the one named last changes fastest.
Arguments:
- tokens: bfloat16 [2048, 4096], P(('ctx', 'tp')), may hold values from -16 to 16
- upstream: bfloat16 [2048, 4096], P('ctx', 'tp'), may hold values from -6 to 6
- w_query: bfloat16 [4096, 4096], P('ctx', 'tp')
- w_keyval: bfloat16 [4096, 2048], P('ctx', 'tp')
- positions: int32 [2048], replicated, may hold values from 0 to 2047, as said below
- documents: int32 [2048], replicated, may hold values from 0 to 3, never falling along the last dimension, each value on 1 to 1024 neighbouring positions
Outputs:
- token_grad: bfloat16 [2048, 4096], P(('ctx', 'tp'))
- query_grad: float32 [4096, 4096], P('ctx', 'tp')
- keyval_grad: float32 [4096, 2048], P('ctx', 'tp')
Inputs may be any that keep to these rules, and one draw needn't show every extreme that they name: Each stored run of 512 tokens holds consecutive increasing positions; the two runs of the tokens of one context rank are the blocks k and 7 - k of the sequence for some k; all runs together hold every position once.
All inputs are finite; a program needn't handle non-finite values.
Results may differ from a plain program's by a relative error of at most 0.02.
The roundings to bfloat16 on the way count: a program that leaves them out, or rounds other values in their place, can miss the bound.
Values may be sent and summed in bfloat16 or wider, within the bound.
No kernel may reach another device: no remote copies, remote signals or barrier semaphores. Data moves between devices by JAX's collectives and lax.ppermute only.
A program may use at most 128 MiB of HBM per device.

v0:
```python
import jax
import jax.numpy as jnp
from jax import lax
from jax.sharding import PartitionSpec as P

KEY_VALUE_HEADS = 8
HEAD_DIMENSION = 128
rope_base = 500000.0


def partner_2(block, axis, bit):
    count = lax.axis_size(axis)
    route = []
    for low in range(count):
        high = low | 1 << bit
        if high != low and high < count:
            route += [(low, high), (high, low)]
    return lax.ppermute(block, axis, route)


def rotation_tables(positions):
    half_width = HEAD_DIMENSION // 2
    frequency = rope_base ** (-(jnp.arange(half_width, dtype=jnp.float32) * 2.0 / HEAD_DIMENSION))
    angles = positions.astype(jnp.float32)[:, None] * frequency[None, :]
    cosine = jnp.concatenate([jnp.cos(angles), jnp.cos(angles)], axis=1)
    sine = jnp.concatenate([jnp.sin(angles), jnp.sin(angles)], axis=1)
    return (cosine, sine)


def rotate(values, cosine, sine):
    half_width = values.shape[-1] // 2
    turned = jnp.concatenate([-values[..., half_width:], values[..., :half_width]], axis=-1)
    return values * cosine[:, None, :] + turned * sine[:, None, :]


def rotate_back(gradient, cosine, sine):
    half_width = gradient.shape[-1] // 2
    scaled = gradient * sine[:, None, :]
    turned = jnp.concatenate([scaled[..., half_width:], -scaled[..., :half_width]], axis=-1)
    return gradient * cosine[:, None, :] + turned


def attend(
    query_rows, grad_out, keys_all, values_all, query_pos, query_doc, key_pos, key_doc, scaling
):
    f32 = jnp.float32
    tok_rows, head_count, head_width = query_rows.shape
    block_rows = min(tok_rows, 128)
    block_count = tok_rows // block_rows
    seq_len = keys_all.shape[0]

    def advance(totals, inputs):
        key_total, value_total = totals
        query_block, grad_block, pos_block, doc_block = inputs
        scores = (
            jnp.einsum("qhd,kd->hqk", query_block, keys_all, preferred_element_type=f32) * scaling
        )
        visible = (key_pos[None, :] <= pos_block[:, None]) & (
            key_doc[None, :] == doc_block[:, None]
        )
        scores = jnp.where(visible[None], scores, -1e30)
        row_peak = jnp.max(scores, axis=-1, keepdims=True)
        exponent = jnp.exp(scores - row_peak)
        probs = exponent / jnp.sum(exponent, axis=-1, keepdims=True)
        probs_half = probs.astype(jnp.bfloat16)
        output = jnp.einsum("hqk,kd->qhd", probs_half, values_all, preferred_element_type=f32)
        deltas = jnp.sum(grad_block.astype(f32) * output, axis=-1)
        prob_grad = jnp.einsum("qhd,kd->hqk", grad_block, values_all, preferred_element_type=f32)
        score_grad = (probs * (prob_grad - deltas.T[:, :, None])).astype(jnp.bfloat16)
        dquery = (
            jnp.einsum("hqk,kd->qhd", score_grad, keys_all, preferred_element_type=f32) * scaling
        )
        key_total = (
            key_total
            + jnp.einsum("hqk,qhd->kd", score_grad, query_block, preferred_element_type=f32)
            * scaling
        )
        value_total = value_total + jnp.einsum(
            "hqk,qhd->kd", probs_half, grad_block, preferred_element_type=f32
        )
        return ((key_total, value_total), dquery)

    blank_keys = jnp.zeros((seq_len, head_width), f32)
    inputs = (
        query_rows.reshape(block_count, block_rows, head_count, head_width),
        grad_out.reshape(block_count, block_rows, head_count, head_width),
        query_pos.reshape(block_count, block_rows),
        query_doc.reshape(block_count, block_rows),
    )
    (key_total, value_total), dquery = lax.scan(advance, (blank_keys, blank_keys), inputs)
    return (dquery.reshape(tok_rows, head_count, head_width), key_total, value_total)


def shards(tokens, upstream, w_query, w_keyval, positions, documents):
    f32 = jnp.float32
    ctx_rank = lax.axis_index("ctx")
    tp_rank = lax.axis_index("tp")
    tensor_split_count = lax.axis_size("tp")
    gathered = lax.all_gather(tokens, "tp", axis=0, tiled=True)
    tok_rows = gathered.shape[0]
    query_cols = w_query.shape[1]
    head_count = query_cols // HEAD_DIMENSION
    pairing_flags = (tensor_split_count // KEY_VALUE_HEADS).bit_length() - 1
    doc_all = jnp.take(documents, positions)
    cosine_all, sine_all = rotation_tables(positions)
    row_offset = ctx_rank * tok_rows
    my_pos = lax.dynamic_slice_in_dim(positions, row_offset, tok_rows, 0)
    my_doc = lax.dynamic_slice_in_dim(doc_all, row_offset, tok_rows, 0)
    my_cos = lax.dynamic_slice_in_dim(cosine_all, row_offset, tok_rows, 0)
    my_sin = lax.dynamic_slice_in_dim(sine_all, row_offset, tok_rows, 0)
    query_full, keyval_full = (
        lax.all_gather(w_query, "ctx", axis=0, tiled=True),
        lax.all_gather(w_keyval, "ctx", axis=0, tiled=True),
    )
    query_raw = jnp.dot(gathered, query_full, preferred_element_type=f32)
    keyval_raw = jnp.dot(gathered, keyval_full, preferred_element_type=f32)
    query_rot = rotate(
        query_raw.reshape(tok_rows, head_count, HEAD_DIMENSION), my_cos, my_sin
    ).astype(jnp.bfloat16)
    head_kv = keyval_raw.astype(jnp.bfloat16)
    for bit_index in range(pairing_flags):
        partner = partner_2(head_kv, "tp", bit_index)
        is_lower = tp_rank // (1 << bit_index) % 2 == 0
        head_kv = jnp.where(
            is_lower,
            jnp.concatenate([head_kv, partner], axis=1),
            jnp.concatenate([partner, head_kv], axis=1),
        )
    key_rot = rotate(head_kv[:, None, :HEAD_DIMENSION].astype(f32), my_cos, my_sin)[:, 0].astype(
        jnp.bfloat16
    )
    local_kv = jnp.concatenate([key_rot, head_kv[:, HEAD_DIMENSION:]], axis=1)
    key_value = lax.all_gather(local_kv, "ctx", axis=0, tiled=True)
    grad_query, grad_key, grad_value = attend(
        query_rot,
        upstream.reshape(tok_rows, head_count, HEAD_DIMENSION),
        key_value[:, :HEAD_DIMENSION],
        key_value[:, HEAD_DIMENSION:],
        my_pos,
        my_doc,
        positions,
        doc_all,
        HEAD_DIMENSION ** (-0.5),
    )
    query_back = (
        rotate_back(grad_query, my_cos, my_sin).astype(jnp.bfloat16).reshape(tok_rows, query_cols)
    )
    key_backward = rotate_back(grad_key[:, None, :], cosine_all, sine_all)[:, 0]
    key_terms = jnp.concatenate([key_backward, grad_value], axis=1)
    head_grad = lax.psum_scatter(
        key_terms.astype(jnp.bfloat16), "ctx", scatter_dimension=0, tiled=True
    ).astype(jnp.float32)
    for bit_index in reversed(range(pairing_flags)):
        half_width = head_grad.shape[1] // 2
        lower_half = head_grad[:, :half_width]
        upper_half = head_grad[:, half_width:]
        is_lower = tp_rank // (1 << bit_index) % 2 == 0
        retained = jnp.where(is_lower, lower_half, upper_half)
        outgoing = jnp.where(is_lower, upper_half, lower_half)
        head_grad = retained + partner_2(outgoing.astype(jnp.bfloat16), "tp", bit_index).astype(
            outgoing.dtype
        )
    key_value_backward = head_grad.astype(jnp.bfloat16)
    row_grads = jnp.concatenate([query_back, key_value_backward], axis=1)
    part_query = lax.dot_general(
        row_grads[:, :query_cols], query_full, (((1,), (1,)), ((), ())), preferred_element_type=f32
    )
    part_keyval = lax.dot_general(
        row_grads[:, query_cols:], keyval_full, (((1,), (1,)), ((), ())), preferred_element_type=f32
    )
    token_grad = lax.psum_scatter(
        (part_query + part_keyval).astype(jnp.bfloat16), "tp", scatter_dimension=0, tiled=True
    )
    weight_grad = lax.psum_scatter(
        lax.dot_general(
            gathered, row_grads, (((0,), (0,)), ((), ())), preferred_element_type=f32
        ).astype(jnp.bfloat16),
        "ctx",
        scatter_dimension=0,
        tiled=True,
    ).astype(jnp.float32)
    return (token_grad, weight_grad[:, :query_cols], weight_grad[:, query_cols:])


def solution(mesh):
    return jax.shard_map(
        shards,
        mesh=mesh,
        in_specs=(P(("ctx", "tp"), None), P("ctx", "tp"), P("ctx", "tp"), P("ctx", "tp"), P(), P()),
        out_specs=(P(("ctx", "tp"), None), P("ctx", "tp"), P("ctx", "tp")),
        check_vma=False,
    )
```

profile of v0, /device:TPU:0, one launch (start us, length us, event | category | flops | bytes accessed | tf_op | source)
XLA Modules:
  0.0 420.0 jit_solution(7259557244311544028)
XLA Ops:
  10.2 11.8 %gather_fusion = s32[2048]{0:T(1024)S(1)} fusion(s32[2048]{0:T(1024)S(1)} %copy-done, s32[2048]{0:T(1024)S(1)} %fusion.52), kind=kCustom, calls=%fused_computation | custom fusion | bytes 24576 | tf_op jit(solution)/shard_map/jit(_take)/gather | solution.py:104
  22.0 1.9 multiply_cosine_fusion
  23.9 23.9 %all-gather.9.cloned.1.call-done = bf16[4096,256]{1,0:T(8,128)(2,1)} async-done(((bf16[1024,256]{1,0:T(8,128)(2,1)}), bf16[4096,256]{1,0:T(8,128)(2,1)}) %all-gather.9.cloned.1.call-update) | async-done | bytes 2097168 | tf_op jit(solution)/shard_map/all_gather | solution.py:113
  47.8 48.5 %all-gather.5.cloned.1.call-done = bf16[512,4096]{1,0:T(8,128)(2,1)} async-done(((bf16[64,4096]{1,0:T(8,128)(2,1)}), bf16[512,4096]{1,0:T(8,128)(2,1)}) %all-gather.5.cloned.1.call-update) | async-done | bytes 4194320 | tf_op jit(solution)/shard_map/all_gather | solution.py:99
  96.3 4.2 convolution_convert_fusion.1
  100.6 0.7 pad_maximum_fusion.3
  101.5 0.9 reshape_reshape.3
  103.2 0.8 copy.28
  104.2 0.8 copy.30
  105.0 44.5 %all-gather.7.cloned.1.call-done = bf16[4096,512]{1,0:T(8,128)(2,1)} async-done(((bf16[1024,512]{1,0:T(8,128)(2,1)}), bf16[4096,512]{1,0:T(8,128)(2,1)}) %all-gather.7.cloned.1.call-update) | async-done | bytes 4194320 | tf_op jit(solution)/shard_map/all_gather | solution.py:112
  149.6 5.8 %fusion.60 = f32[512,512]{0,1:T(8,128)S(1)} fusion(bf16[512,4096]{1,0:T(8,128)(2,1)} %all-gather.5.cloned.1.call-done, bf16[4096,512]{1,0:T(8,128)(2,1)} %all-gather.7.cloned.1.call-done), kind=kOutput, calls=%fused_computation.102 | convolution fusion | flops 2147483648 | bytes 9437184 | tf_op jit(solution)/shard_map/dot_general | solution.py:115
  156.3 1.5 fusion.42
  158.1 19.5 %all-gather.11.cloned.1.call-done = bf16[2048,256]{0,1:T(8,128)(2,1)} async-done(((bf16[512,256]{0,1:T(8,128)(2,1)}), bf16[2048,256]{0,1:T(8,128)(2,1)}) %all-gather.11.cloned.1.call-update) | async-done | bytes 1048592 | tf_op jit(solution)/shard_map/all_gather | solution.py:133
  177.7 2.1 fusion.58
  180.0 63.6 %while.15 = (s32[]{:T(128)}, f32[2048,128]{1,0:T(8,128)}, f32[2048,128]{1,0:T(8,128)}, f32[4,128,4,128]{3,1,2,0:T(8,128)}, s32[2048]{0:T(1024)S(1)}, /*index=5*/...) while((s32[]{:T(128)}, f32[2048,128]{1,0:T(8,128)}, ...), condition=%wide.region_4.5_spmd.clone, body=%wide.region_0.4_spmd.clone.sunk | while | flops 1625556480 | bytes 52066004 | solution.py:90
  181.2 0.7 fusion.104
  181.9 1.9 fusion.106
  184.5 1.0 constant_dynamic-slice_fusion.4
  185.4 0.8 fusion.108
  186.2 2.1 fusion.109
  188.3 3.5 fusion.110
  191.8 1.4 fusion.112
  193.2 1.8 fusion.111
  195.9 0.7 fusion.104
  196.6 1.9 fusion.106
  199.2 1.0 constant_dynamic-slice_fusion.4
  200.2 0.8 fusion.108
  200.9 2.1 fusion.109
  203.0 3.7 fusion.110
  206.8 1.4 fusion.112
  208.2 3.0 fusion.111
  212.1 0.7 fusion.104
  212.9 1.9 fusion.106
  215.4 1.0 constant_dynamic-slice_fusion.4
  216.4 0.8 fusion.108
  217.2 2.1 fusion.109
  219.3 3.7 fusion.110
  223.0 1.4 fusion.112
  224.4 3.0 fusion.111
  228.4 0.7 fusion.104
  229.1 1.9 fusion.106
  231.6 1.0 constant_dynamic-slice_fusion.4
  232.6 0.8 fusion.108
  233.4 2.1 fusion.109
  235.5 3.7 fusion.110
  239.2 1.4 fusion.112
  240.6 3.0 fusion.111
  243.6 1.6 copy.39
  245.2 1.4 fusion.35
  246.6 0.9 slice_bitcast_fusion
  247.5 2.3 copy.41
  249.8 1.3 fusion.38
  251.1 2.2 pad_maximum_fusion.2
  255.3 26.1 %reduce-scatter.4.cloned.1.call-done = bf16[512,256]{0,1:T(8,128)(2,1)} async-done(((bf16[2048,256]{0,1:T(8,128)(2,1)}), bf16[512,256]{0,1:T(8,128)(2,1)}) %reduce-scatter.4.cloned.1.call-update) | async-done | bytes 262160 | tf_op jit(solution)/shard_map/reduce_scatter | solution.py:150
  281.4 1.1 copy.42
  282.5 7.6 %fusion.33 = bf16[4096,768]{0,1:T(8,128)(2,1)} fusion(bf16[512,4096]{1,0:T(8,128)(2,1)} %all-gather.5.cloned.1.call-done, bf16[512,256]{1,0:T(8,128)(2,1)S(1)} %copy.42, bf16[512,512]{1,0:T(8,128)(2,1)S(1)} %fusion.40), kind=kOutput, calls=%fused_computation.48 | convolution fusion | flops 3225944064 | bytes 11272192 | tf_op jit(solution)/shard_map/dot_general | solution.py:175
  290.4 4.7 %fusion.61 = f32[512,4096]{1,0:T(8,128)S(1)} fusion(bf16[512,512]{1,0:T(8,128)(2,1)S(1)} %fusion.40, bf16[4096,512]{1,0:T(8,128)(2,1)} %all-gather.7.cloned.1.call-done), kind=kOutput, calls=%fused_computation.103 | convolution fusion | flops 2147483648 | bytes 13107200 | tf_op jit(solution)/shard_map/dot_general | solution.py:165
  295.2 3.5 add_convert_fusion
  298.7 61.6 %reduce-scatter.8.cloned.1.call-done = bf16[1024,768]{0,1:T(8,128)(2,1)} async-done(((bf16[4096,768]{0,1:T(8,128)(2,1)}), bf16[1024,768]{0,1:T(8,128)(2,1)}) %reduce-scatter.8.cloned.1.call-update) | async-done | bytes 1572880 | tf_op jit(solution)/shard_map/reduce_scatter | solution.py:174
  360.3 1.5 slice.70
  361.8 1.8 copy.43
  363.6 1.1 slice.71
  364.8 1.3 copy.44
  366.1 47.1 %reduce-scatter.6.cloned.1.call-done = bf16[64,4096]{1,0:T(8,128)(2,1)} async-done(((bf16[512,4096]{1,0:T(8,128)(2,1)}), bf16[64,4096]{1,0:T(8,128)(2,1)}) %reduce-scatter.6.cloned.1.call-update) | async-done | bytes 524304 | tf_op jit(solution)/shard_map/reduce_scatter | solution.py:171
  (90 shorter events, 14.3 us)
Async XLA Ops:
  7.2 3.0 copy-start
  7.2 40.6 %all-gather.9.cloned.1.call-start = ((), (), s32[]{:S(2)}) async-start(), calls=%async_computation.5 | async-start | bytes 2621440 | tf_op jit(solution)/shard_map/all_gather | solution.py:113
  7.9 88.3 %all-gather.5.cloned.1.call-start = ((), (), s32[]{:S(2)}) async-start(), calls=%async_computation.3 | async-start | bytes 4718592 | tf_op jit(solution)/shard_map/all_gather | solution.py:99
  8.7 140.9 %all-gather.7.cloned.1.call-start = ((), (), s32[]{:S(2)}) async-start(), calls=%async_computation.4 | async-start | bytes 5242880 | tf_op jit(solution)/shard_map/all_gather | solution.py:112
  9.4 168.3 %all-gather.11.cloned.1.call-start = ((), (), s32[]{:S(2)}) async-start(), calls=%async_computation.6 | async-start | bytes 1310720 | tf_op jit(solution)/shard_map/all_gather | solution.py:133
  10.2 11.8 %copy-start.13 = (s32[2048]{0:T(1024)S(1)}, s32[2048]{0:T(1024)}, u32[]{:S(2)}) copy-start(s32[2048]{0:T(1024)} %param.12) | copy-start | bytes 24580
  23.9 76.6 %copy-start.3 = (f32[2048,64]{0,1:T(8,128)}, f32[2048,64]{0,1:T(8,128)S(1)}, u32[]{:S(2)}) copy-start(f32[2048,64]{0,1:T(8,128)S(1)} %get-tuple-element.183) | copy-start | bytes 1572868
  23.9 76.6 %copy-start.4 = (f32[2048,64]{0,1:T(8,128)}, f32[2048,64]{0,1:T(8,128)S(1)}, u32[]{:S(2)}) copy-start(f32[2048,64]{0,1:T(8,128)S(1)} %get-tuple-element.182) | copy-start | bytes 1572868
  100.4 1.0 copy-start.11
  101.4 180.0 %reduce-scatter.4.cloned.1.call-start = ((), (), s32[]{:S(2)}) async-start(), calls=%async_computation.7 | async-start | bytes 1310720 | tf_op jit(solution)/shard_map/reduce_scatter | solution.py:150
  104.2 45.4 %copy-start.7 = (f32[512,128]{1,0:T(8,128)}, f32[512,128]{1,0:T(8,128)S(1)}, u32[]{:S(2)}) copy-start(f32[512,128]{1,0:T(8,128)S(1)} %copy.29) | copy-start | bytes 786436
  183.8 1.6 copy-start.12
  188.3 3.5 copy-start.2
  198.5 1.6 copy-start.12
  203.0 3.7 copy-start.2
  214.8 1.6 copy-start.12
  219.3 3.7 copy-start.2
  231.0 1.6 copy-start.12
  235.5 3.7 copy-start.2
  243.6 6.2 %copy-start.5 = (f32[2048,64]{0,1:T(8,128)S(1)}, f32[2048,64]{0,1:T(8,128)}, u32[]{:S(2)}) copy-start(f32[2048,64]{0,1:T(8,128)} %copy-done.4) | copy-start | bytes 1572868
  247.5 5.9 %copy-start.6 = (f32[4,128,4,128]{3,1,2,0:T(8,128)S(1)}, f32[4,128,4,128]{3,1,2,0:T(8,128)}, u32[]{:S(2)}) copy-start(f32[4,128,4,128]{3,1,2,0:T(8,128)} %get-tuple-element.67) | copy-start | bytes 3145732
  251.1 3.1 copy-start.8
  253.3 107.0 %reduce-scatter.8.cloned.1.call-start = ((), (), s32[]{:S(2)}) async-start(), calls=%async_computation.9 | async-start | bytes 7864320 | tf_op jit(solution)/shard_map/reduce_scatter | solution.py:174
  290.2 5.0 %copy-start.9 = (bf16[4096,256]{1,0:T(8,128)(2,1)S(1)}, bf16[4096,256]{1,0:T(8,128)(2,1)}, u32[]{:S(2)}) copy-start(bf16[4096,256]{1,0:T(8,128)(2,1)} %all-gather.9.cloned.1.call-done) | copy-start | bytes 6291460
  290.2 5.0 %copy-start.10 = (bf16[512,256]{0,1:T(8,128)(2,1)S(1)}, bf16[512,256]{0,1:T(8,128)(2,1)}, u32[]{:S(2)}) copy-start(bf16[512,256]{0,1:T(8,128)(2,1)} %reduce-scatter.4.cloned.1.call-done) | copy-start | bytes 786436
  290.2 123.0 %reduce-scatter.6.cloned.1.call-start = ((), (), s32[]{:S(2)}) async-start(), calls=%async_computation.8 | async-start | bytes 4718592 | tf_op jit(solution)/shard_map/reduce_scatter | solution.py:171
  360.3 52.8 %copy-start.1 = (s32[2048]{0:T(1024)S(1)}, s32[2048]{0:T(1024)}, u32[]{:S(2)}) copy-start(s32[2048]{0:T(1024)} %param.13) | copy-start | bytes 24580
Sparse Core Ops, SparseCore 0:
  9.8 37.8 all-gather.8
  49.4 46.8 all-gather.4
  98.1 51.4 all-gather.6
  151.3 26.3 all-gather.10
  253.5 27.9 reduce-scatter.3
  290.3 70.0 reduce-scatter.7
  363.2 49.9 reduce-scatter.5
where the time goes:
time: 421 us; the launch traced here: 420 us
  waiting for transfers between devices  273 us (65%)
  matrix products  71.2 us (17%)
  local copies, waits for them, and re-layouts  37.1 us (9%)
  other arithmetic  23 us (5%)
  between operations  14.5 us (3%)
    reduce_scatter x1, waiting for transfers between devices, shards(): lax.psum_scatter(lax.dot_general(gathered, row_grads, (((0,), (0,)), ((),...  61.6 us
    all_gather x1, waiting for transfers between devices, shards(): gathered = lax.all_gather(tokens, 'tp', axis=0, tiled=True)  48.5 us
    reduce_scatter x1, waiting for transfers between devices, shards(): lax.psum_scatter((part_query + part_keyval).astype(jnp.bfloat16), 'tp', s...  47.1 us
    all_gather x1, waiting for transfers between devices, shards(): lax.all_gather(w_query, 'ctx', axis=0, tiled=True)  44.5 us
    reduce_scatter x1, waiting for transfers between devices, shards(): lax.psum_scatter(key_terms.astype(jnp.bfloat16), 'ctx', scatter_dimension...  26.1 us
    all_gather x1, waiting for transfers between devices, shards(): lax.all_gather(w_keyval, 'ctx', axis=0, tiled=True)  23.9 us
    all_gather x1, waiting for transfers between devices, shards(): key_value = lax.all_gather(local_kv, 'ctx', axis=0, tiled=True)  19.5 us
    dot_general x4, matrix products, advance(): jnp.einsum('hqk,qhd->kd', score_grad, query_block, preferred_element_type...  14.6 us
  transfers between devices with their start and end apart: 7, of which 7 were waited for; matrix products, arithmetic and copies ran while one was open for 11% of the time, Pallas kernels for 0%

commit v1 on v0

--- a/solution.py
+++ b/solution.py
@@ -6,6 +6,17 @@
 KEY_VALUE_HEADS = 8
 HEAD_DIMENSION = 128
 rope_base = 500000.0
+
+
+def turned_line(shard, mesh_axis, along):
+    devices = lax.axis_size(mesh_axis)
+    hops = [(i, (i + 1) % devices) for i in range(devices)]
+    parts = [shard]
+    for far in range(1, devices):
+        parts = [lax.ppermute(parts[0], mesh_axis, hops), *parts]
+    whole = jnp.concatenate(parts, axis=along)
+    shift = (lax.axis_index(mesh_axis) + 1) * parts[-1].shape[along]
+    return jnp.roll(whole, shift, axis=along)
 
 
 def partner_2(block, axis, bit):
@@ -96,7 +107,7 @@
     ctx_rank = lax.axis_index("ctx")
     tp_rank = lax.axis_index("tp")
     tensor_split_count = lax.axis_size("tp")
-    gathered = lax.all_gather(tokens, "tp", axis=0, tiled=True)
+    gathered = turned_line(tokens, "tp", 0)
     tok_rows = gathered.shape[0]
     query_cols = w_query.shape[1]
     head_count = query_cols // HEAD_DIMENSION

time: 421 us -> 440 us (1.045)
  local copies, waits for them, and re-layouts: 37.1 us -> 55.2 us
    ppermute x0 -> x7, waiting for transfers between devices: none -> 61.5 us  [turned_line(): parts = [lax.ppermute(parts[0], mesh_axis, hops), *parts]]
    all_gather x1 -> x0, waiting for transfers between devices: 48.5 us -> none  [shards(): gathered = lax.all_gather(tokens, 'tp', axis=0, tiled=True)]
    all_gather x1, waiting for transfers between devices: 23.9 us -> 0.01 us  [shards(): lax.all_gather(w_keyval, 'ctx', axis=0, tiled=True)]
    unnamed x28 -> x49, local copies, waits for them, and re-layouts: 3.84 us -> 18.6 us
    all_gather x1, waiting for transfers between devices: 44.5 us -> 52.1 us  [shards(): lax.all_gather(w_query, 'ctx', axis=0, tiled=True)]
  transfers between devices with their start and end apart: 7 -> 13, of which waited for: 7 -> 11; matrix products, arithmetic and copies ran while one was open for 11% -> 12% of each run, Pallas kernels for 0% -> 0%
where the time goes in v1:
time: 440 us; the launch traced here: 438 us
  waiting for transfers between devices  272 us (62%)
  matrix products  72 us (16%)
  local copies, waits for them, and re-layouts  55.2 us (13%)
  other arithmetic  23.8 us (5%)
  between operations  14.5 us (3%)
    reduce_scatter x1, waiting for transfers between devices, shards(): lax.psum_scatter(lax.dot_general(gathered, row_grads, (((0,), (0,)), ((),...  61.8 us
    ppermute x7, waiting for transfers between devices, turned_line(): parts = [lax.ppermute(parts[0], mesh_axis, hops), *parts]  61.5 us
    all_gather x1, waiting for transfers between devices, shards(): lax.all_gather(w_query, 'ctx', axis=0, tiled=True)  52.1 us
    reduce_scatter x1, waiting for transfers between devices, shards(): lax.psum_scatter((part_query + part_keyval).astype(jnp.bfloat16), 'tp', s...  48.7 us
    reduce_scatter x1, waiting for transfers between devices, shards(): lax.psum_scatter(key_terms.astype(jnp.bfloat16), 'ctx', scatter_dimension...  25.9 us
    all_gather x1, waiting for transfers between devices, shards(): key_value = lax.all_gather(local_kv, 'ctx', axis=0, tiled=True)  20.9 us
    unnamed x49, local copies, waits for them, and re-layouts  18.6 us
    dot_general x4, matrix products, advance(): jnp.einsum('hqk,qhd->kd', score_grad, query_block, preferred_element_type...  14.6 us
  transfers between devices with their start and end apart: 13, of which 11 were waited for; matrix products, arithmetic and copies ran while one was open for 12% of the time, Pallas kernels for 0%

profile of v1, /device:TPU:0, one launch (start us, length us, event | category | flops | bytes accessed | tf_op | source)
XLA Modules:
  0.0 438.5 jit_solution(3136624606851854081)
XLA Ops:
  7.8 11.1 %collective-permute-done = bf16[64,4096]{1,0:T(8,128)(2,1)S(1)} collective-permute-done((bf16[64,4096]{1,0:T(8,128)(2,1)}, bf16[64,4096]{1,0:T(8,128)(2,1)S(1)}, u32[]{:S(2)}, u32[]{:S(2)}) %collective-permute-start) | collective-permute-done | bytes 524320 | tf_op jit(solution)/shard_map/ppermute | solution.py:16
  18.9 10.4 %collective-permute-done.1 = bf16[64,4096]{1,0:T(8,128)(2,1)S(1)} collective-permute-done((bf16[64,4096]{1,0:T(8,128)(2,1)S(1)}, bf16[64,4096]{1,0:T(8,128)(2,1)S(1)}, u32[]{:S(2)}, u32[]{:S(2)}) %collective-permute-start.1) | collective-permute-done | bytes 524320 | tf_op jit(solution)/shard_map/ppermute | solution.py:16
  29.3 10.4 %collective-permute-done.2 = bf16[64,4096]{1,0:T(8,128)(2,1)S(1)} collective-permute-done((bf16[64,4096]{1,0:T(8,128)(2,1)S(1)}, bf16[64,4096]{1,0:T(8,128)(2,1)S(1)}, u32[]{:S(2)}, u32[]{:S(2)}) %collective-permute-start.2) | collective-permute-done | bytes 524320 | tf_op jit(solution)/shard_map/ppermute | solution.py:16
  39.7 10.4 %collective-permute-done.3 = bf16[64,4096]{1,0:T(8,128)(2,1)S(1)} collective-permute-done((bf16[64,4096]{1,0:T(8,128)(2,1)S(1)}, bf16[64,4096]{1,0:T(8,128)(2,1)S(1)}, u32[]{:S(2)}, u32[]{:S(2)}) %collective-permute-start.3) | collective-permute-done | bytes 524320 | tf_op jit(solution)/shard_map/ppermute | solution.py:16
  50.1 10.4 %collective-permute-done.4 = bf16[64,4096]{1,0:T(8,128)(2,1)S(1)} collective-permute-done((bf16[64,4096]{1,0:T(8,128)(2,1)S(1)}, bf16[64,4096]{1,0:T(8,128)(2,1)S(1)}, u32[]{:S(2)}, u32[]{:S(2)}) %collective-permute-start.4) | collective-permute-done | bytes 524320 | tf_op jit(solution)/shard_map/ppermute | solution.py:16
  61.3 11.8 %gather_fusion = s32[2048]{0:T(1024)S(1)} fusion(s32[2048]{0:T(1024)S(1)} %copy-done, s32[2048]{0:T(1024)S(1)} %fusion.59), kind=kCustom, calls=%fused_computation | custom fusion | bytes 24576 | tf_op jit(solution)/shard_map/jit(_take)/gather | solution.py:115
  73.3 1.9 multiply_cosine_fusion
  75.2 8.7 %collective-permute-done.6 = bf16[64,4096]{1,0:T(8,128)(2,1)} collective-permute-done((bf16[64,4096]{1,0:T(8,128)(2,1)}, bf16[64,4096]{1,0:T(8,128)(2,1)}, u32[]{:S(2)}, u32[]{:S(2)}) %collective-permute-start.6) | collective-permute-done | bytes 524320 | tf_op jit(solution)/shard_map/ppermute | solution.py:16
  83.9 1.9 constant_dynamic-update-slice_fusion.15
  85.8 1.9 constant_dynamic-update-slice_fusion.14
  87.7 1.9 constant_dynamic-update-slice_fusion.13
  93.8 1.9 constant_dynamic-update-slice_fusion.7
  95.7 1.9 constant_dynamic-update-slice_fusion.6
  100.9 0.9 constant_dynamic-update-slice_fusion.1
  101.8 0.9 constant_dynamic-update-slice_fusion
  102.7 4.2 fusion.38
  108.6 0.9 reshape_reshape.3
  112.1 20.9 %all-gather.8.cloned.1.call-done = bf16[2048,256]{0,1:T(8,128)(2,1)} async-done(((bf16[512,256]{0,1:T(8,128)(2,1)}), bf16[2048,256]{0,1:T(8,128)(2,1)}) %all-gather.8.cloned.1.call-update) | async-done | bytes 1048592 | tf_op jit(solution)/shard_map/all_gather | solution.py:144
  133.0 2.1 fusion.68
  135.4 52.1 %all-gather.4.cloned.1.call-done = bf16[4096,512]{1,0:T(8,128)(2,1)} async-done(((bf16[1024,512]{1,0:T(8,128)(2,1)}), bf16[4096,512]{1,0:T(8,128)(2,1)}) %all-gather.4.cloned.1.call-update) | async-done | bytes 4194320 | tf_op jit(solution)/shard_map/all_gather | solution.py:123
  187.4 5.8 %fusion.36 = f32[512,512]{0,1:T(8,128)S(1)} fusion(bf16[4096,512]{1,0:T(8,128)(2,1)} %all-gather.4.cloned.1.call-done, bf16[1024,4096]{1,0:T(8,128)(2,1)} %constant_dynamic-update-slice_fusion, s32[]{:T(128)S(6)} %select_n.39), kind=kOutput, calls=%fused_computation.51 | convolution fusion | flops 2147483648 | bytes 9437188 | tf_op jit(solution)/shard_map/dot_general | solution.py:126
  193.7 0.9 slice_negate_fusion.2
  194.6 1.2 concatenate.53
  196.0 1.5 fusion.49
  197.8 63.7 %while.15 = (s32[]{:T(128)}, f32[2048,128]{1,0:T(8,128)}, f32[2048,128]{1,0:T(8,128)}, f32[4,128,4,128]{3,1,2,0:T(8,128)}, s32[2048]{0:T(1024)S(1)}, /*index=5*/...) while((s32[]{:T(128)}, f32[2048,128]{1,0:T(8,128)}, ...), condition=%wide.region_4.5_spmd.clone, body=%wide.region_0.4_spmd.clone.sunk | while | flops 1625556480 | bytes 52066004 | solution.py:101
  199.7 1.9 fusion.112
  202.3 1.0 constant_dynamic-slice_fusion.4
  204.0 2.1 fusion.115
  206.1 3.5 fusion.116
  209.6 1.4 fusion.118
  211.0 1.8 fusion.117
  214.5 1.9 fusion.112
  217.0 1.0 constant_dynamic-slice_fusion.4
  218.8 2.1 fusion.115
  220.9 3.7 fusion.116
  224.6 1.4 fusion.118
  226.0 3.0 fusion.117
  230.7 1.9 fusion.112
  233.2 1.0 constant_dynamic-slice_fusion.4
  235.0 2.1 fusion.115
  237.1 3.7 fusion.116
  240.8 1.4 fusion.118
  242.2 3.0 fusion.117
  246.9 1.9 fusion.112
  249.5 1.0 constant_dynamic-slice_fusion.4
  251.2 2.1 fusion.115
  253.3 3.7 fusion.116
  257.1 1.4 fusion.118
  258.5 3.0 fusion.117
  261.5 1.6 copy.37
  263.1 1.4 fusion.42
  264.5 0.9 slice_bitcast_fusion
  265.4 2.3 copy.39
  267.7 1.3 fusion.45
  269.0 2.2 pad_maximum_fusion.2
  273.4 25.9 %reduce-scatter.4.cloned.1.call-done = bf16[512,256]{0,1:T(8,128)(2,1)} async-done(((bf16[2048,256]{0,1:T(8,128)(2,1)}), bf16[512,256]{0,1:T(8,128)(2,1)}) %reduce-scatter.4.cloned.1.call-update) | async-done | bytes 262160 | tf_op jit(solution)/shard_map/reduce_scatter | solution.py:161
  299.3 1.1 copy.40
  300.4 8.4 %convolution_convert_fusion = bf16[4096,768]{1,0:T(8,128)(2,1)} fusion(bf16[1024,4096]{1,0:T(8,128)(2,1)} %constant_dynamic-update-slice_fusion, s32[]{:T(128)S(6)} %select_n.39, bf16[512,256]{1,0:T(8,128)(2,1)S(1)} %copy.40, bf16[512,512]{1,0:T(8,128)(2,1)S(1)} %fusion.47), kind=kOutput, calls=%fused_computation.47 | convolution fusion | flops 3225944064 | bytes 11272196 | tf_op jit(solution)/shard_map/dot_general | solution.py:186
  308.9 4.7 %fusion.70 = f32[512,4096]{1,0:T(8,128)S(1)} fusion(bf16[512,512]{1,0:T(8,128)(2,1)S(1)} %fusion.47, bf16[4096,512]{1,0:T(8,128)(2,1)} %all-gather.4.cloned.1.call-done), kind=kOutput, calls=%fused_computation.125 | convolution fusion | flops 2147483648 | bytes 13107200 | tf_op jit(solution)/shard_map/dot_general | solution.py:176
  313.6 3.5 add_convert_fusion
  317.1 61.8 %reduce-scatter.8.cloned.1.call-done = bf16[1024,768]{1,0:T(8,128)(2,1)} async-done(((bf16[4096,768]{1,0:T(8,128)(2,1)}), bf16[1024,768]{1,0:T(8,128)(2,1)}) %reduce-scatter.8.cloned.1.call-update) | async-done | bytes 1572880 | tf_op jit(solution)/shard_map/reduce_scatter | solution.py:185
  379.0 3.0 slice.70
  381.9 1.0 slice.71
  383.0 48.7 %reduce-scatter.6.cloned.1.call-done = bf16[64,4096]{1,0:T(8,128)(2,1)} async-done(((bf16[512,4096]{1,0:T(8,128)(2,1)}), bf16[64,4096]{1,0:T(8,128)(2,1)}) %reduce-scatter.6.cloned.1.call-update) | async-done | bytes 524304 | tf_op jit(solution)/shard_map/reduce_scatter | solution.py:182
  (123 shorter events, 29.2 us)
Async XLA Ops:
  7.2 54.1 %copy-start = (s32[2048]{0:T(1024)S(1)}, s32[2048]{0:T(1024)}, u32[]{:S(2)}) copy-start(s32[2048]{0:T(1024)} %param.13) | copy-start | bytes 24580
  7.2 95.5 %all-gather.6.cloned.1.call-start = ((), (), s32[]{:S(2)}) async-start(), calls=%async_computation.4 | async-start | bytes 2621440 | tf_op jit(solution)/shard_map/all_gather | solution.py:124
  7.2 11.6 %collective-permute-start = (bf16[64,4096]{1,0:T(8,128)(2,1)}, bf16[64,4096]{1,0:T(8,128)(2,1)S(1)}, u32[]{:S(2)}, u32[]{:S(2)}) collective-permute-start(bf16[64,4096]{1,0:T(8,128)(2,1)} %param.8), channel_id=1, source_target_pairs={{0,1},{1,2},{2,3},{3,4},{4,5},{5,6},{6,7},{7,0},{8,9},{9,10},{10,1... | collective-permute-start | bytes 1572872 | tf_op jit(solution)/shard_map/ppermute | solution.py:16
  18.9 10.4 %collective-permute-start.1 = (bf16[64,4096]{1,0:T(8,128)(2,1)S(1)}, bf16[64,4096]{1,0:T(8,128)(2,1)S(1)}, u32[]{:S(2)}, u32[]{:S(2)}) collective-permute-start(bf16[64,4096]{1,0:T(8,128)(2,1)S(1)} %collective-permute-done), channel_id=1, source_target_pairs={{0,1},{1,2},{2,3},{3,4},{4,5},{5,6},{6,7},{7,0},{8,9},{9,10},{10,1... | collective-permute-start | bytes 1572872 | tf_op jit(solution)/shard_map/ppermute | solution.py:16
  29.3 10.4 %collective-permute-start.2 = (bf16[64,4096]{1,0:T(8,128)(2,1)S(1)}, bf16[64,4096]{1,0:T(8,128)(2,1)S(1)}, u32[]{:S(2)}, u32[]{:S(2)}) collective-permute-start(bf16[64,4096]{1,0:T(8,128)(2,1)S(1)} %collective-permute-done.1), channel_id=1, source_target_pairs={{0,1},{1,2},{2,3},{3,4},{4,5},{5,6},{6,7},{7,0},{8,9},{9,10},{10,1... | collective-permute-start | bytes 1572872 | tf_op jit(solution)/shard_map/ppermute | solution.py:16
  39.7 10.4 %collective-permute-start.3 = (bf16[64,4096]{1,0:T(8,128)(2,1)S(1)}, bf16[64,4096]{1,0:T(8,128)(2,1)S(1)}, u32[]{:S(2)}, u32[]{:S(2)}) collective-permute-start(bf16[64,4096]{1,0:T(8,128)(2,1)S(1)} %collective-permute-done.2), channel_id=1, source_target_pairs={{0,1},{1,2},{2,3},{3,4},{4,5},{5,6},{6,7},{7,0},{8,9},{9,10},{10,1... | collective-permute-start | bytes 1572872 | tf_op jit(solution)/shard_map/ppermute | solution.py:16
  50.1 10.4 %collective-permute-start.4 = (bf16[64,4096]{1,0:T(8,128)(2,1)S(1)}, bf16[64,4096]{1,0:T(8,128)(2,1)S(1)}, u32[]{:S(2)}, u32[]{:S(2)}) collective-permute-start(bf16[64,4096]{1,0:T(8,128)(2,1)S(1)} %collective-permute-done.3), channel_id=1, source_target_pairs={{0,1},{1,2},{2,3},{3,4},{4,5},{5,6},{6,7},{7,0},{8,9},{9,10},{10,1... | collective-permute-start | bytes 1572872 | tf_op jit(solution)/shard_map/ppermute | solution.py:16
  60.5 12.6 %copy-start.12 = (bf16[64,4096]{1,0:T(8,128)(2,1)}, bf16[64,4096]{1,0:T(8,128)(2,1)S(1)}, u32[]{:S(2)}) copy-start(bf16[64,4096]{1,0:T(8,128)(2,1)S(1)} %collective-permute-done.4) | copy-start | bytes 1572868
  60.5 12.6 %collective-permute-start.5 = (bf16[64,4096]{1,0:T(8,128)(2,1)S(1)}, bf16[64,4096]{1,0:T(8,128)(2,1)}, u32[]{:S(2)}, u32[]{:S(2)}) collective-permute-start(bf16[64,4096]{1,0:T(8,128)(2,1)S(1)} %collective-permute-done.4), channel_id=1, source_target_pairs={{0,1},{1,2},{2,3},{3,4},{4,5},{5,6},{6,7},{7,0},{8,9},{9,10},{10,1... | collective-permute-start | bytes 1572872 | tf_op jit(solution)/shard_map/ppermute | solution.py:16
  60.5 72.5 %all-gather.8.cloned.1.call-start = ((), (), s32[]{:S(2)}) async-start(), calls=%async_computation.5 | async-start | bytes 1310720 | tf_op jit(solution)/shard_map/all_gather | solution.py:144
  61.3 11.8 %copy-start.17 = (s32[2048]{0:T(1024)S(1)}, s32[2048]{0:T(1024)}, u32[]{:S(2)}) copy-start(s32[2048]{0:T(1024)} %param.12) | copy-start | bytes 24580
  73.1 10.8 %collective-permute-start.6 = (bf16[64,4096]{1,0:T(8,128)(2,1)}, bf16[64,4096]{1,0:T(8,128)(2,1)}, u32[]{:S(2)}, u32[]{:S(2)}) collective-permute-start(bf16[64,4096]{1,0:T(8,128)(2,1)} %collective-permute-done.5), channel_id=1, source_target_pairs={{0,1},{1,2},{2,3},{3,4},{4,5},{5,6},{6,7},{7,0},{8,9},{9,10},{10,1... | collective-permute-start | bytes 1572872 | tf_op jit(solution)/shard_map/ppermute | solution.py:16
  73.3 19.7 %copy-start.11 = (bf16[64,4096]{1,0:T(8,128)(2,1)S(1)}, bf16[64,4096]{1,0:T(8,128)(2,1)}, u32[]{:S(2)}) copy-start(bf16[64,4096]{1,0:T(8,128)(2,1)} %param.8) | copy-start | bytes 1572868
  75.2 31.8 %copy-start.4 = (f32[2048,64]{0,1:T(8,128)}, f32[2048,64]{0,1:T(8,128)S(1)}, u32[]{:S(2)}) copy-start(f32[2048,64]{0,1:T(8,128)S(1)} %get-tuple-element.177) | copy-start | bytes 1572868
  75.2 31.8 %copy-start.5 = (f32[2048,64]{0,1:T(8,128)}, f32[2048,64]{0,1:T(8,128)S(1)}, u32[]{:S(2)}) copy-start(f32[2048,64]{0,1:T(8,128)S(1)} %get-tuple-element.176) | copy-start | bytes 1572868
  87.7 9.9 %copy-start.13 = (bf16[64,4096]{1,0:T(8,128)(2,1)S(1)}, bf16[64,4096]{1,0:T(8,128)(2,1)}, u32[]{:S(2)}) copy-start(bf16[64,4096]{1,0:T(8,128)(2,1)} %copy-done.12) | copy-start | bytes 1572868
  106.8 1.8 copy-start.15
  107.8 79.7 %all-gather.4.cloned.1.call-start = ((), (), s32[]{:S(2)}) async-start(), calls=%async_computation.3 | async-start | bytes 5242880 | tf_op jit(solution)/shard_map/all_gather | solution.py:123
  108.5 190.8 %reduce-scatter.4.cloned.1.call-start = ((), (), s32[]{:S(2)}) async-start(), calls=%async_computation.6 | async-start | bytes 1310720 | tf_op jit(solution)/shard_map/reduce_scatter | solution.py:161
  111.3 23.8 %copy-start.8 = (f32[512,128]{1,0:T(8,128)}, f32[512,128]{1,0:T(8,128)S(1)}, u32[]{:S(2)}) copy-start(f32[512,128]{1,0:T(8,128)S(1)} %copy.27) | copy-start | bytes 786436
  201.6 1.6 copy-start.16
  206.1 3.5 copy-start.2
  216.3 1.6 copy-start.16
  220.9 3.7 copy-start.2
  232.6 1.6 copy-start.16
  237.1 3.7 copy-start.2
  248.8 1.6 copy-start.16
  253.3 3.7 copy-start.2
  261.5 6.2 %copy-start.6 = (f32[2048,64]{0,1:T(8,128)S(1)}, f32[2048,64]{0,1:T(8,128)}, u32[]{:S(2)}) copy-start(f32[2048,64]{0,1:T(8,128)} %copy-done.5) | copy-start | bytes 1572868
  265.4 6.1 %copy-start.7 = (f32[4,128,4,128]{3,1,2,0:T(8,128)S(1)}, f32[4,128,4,128]{3,1,2,0:T(8,128)}, u32[]{:S(2)}) copy-start(f32[4,128,4,128]{3,1,2,0:T(8,128)} %get-tuple-element.67) | copy-start | bytes 3145732
  268.9 3.3 copy-start.9
  271.2 107.8 %reduce-scatter.8.cloned.1.call-start = ((), (), s32[]{:S(2)}) async-start(), calls=%async_computation.8 | async-start | bytes 7864320 | tf_op jit(solution)/shard_map/reduce_scatter | solution.py:185
  308.8 4.8 %copy-start.10 = (bf16[4096,256]{1,0:T(8,128)(2,1)S(1)}, bf16[4096,256]{1,0:T(8,128)(2,1)}, u32[]{:S(2)}) copy-start(bf16[4096,256]{1,0:T(8,128)(2,1)} %all-gather.6.cloned.1.call-done) | copy-start | bytes 6291460
  308.8 4.8 %copy-start.14 = (bf16[512,256]{0,1:T(8,128)(2,1)S(1)}, bf16[512,256]{0,1:T(8,128)(2,1)}, u32[]{:S(2)}) copy-start(bf16[512,256]{0,1:T(8,128)(2,1)} %reduce-scatter.4.cloned.1.call-done) | copy-start | bytes 786436
  308.8 122.8 %reduce-scatter.6.cloned.1.call-start = ((), (), s32[]{:S(2)}) async-start(), calls=%async_computation.7 | async-start | bytes 4718592 | tf_op jit(solution)/shard_map/reduce_scatter | solution.py:182
  317.1 114.5 %copy-start.1 = (s32[2048]{0:T(1024)S(1)}, s32[2048]{0:T(1024)}, u32[]{:S(2)}) copy-start(s32[2048]{0:T(1024)} %param.13) | copy-start | bytes 24580
  379.0 3.0 copy-start.3
Sparse Core Ops, SparseCore 0:
  60.6 36.8 all-gather.5
  107.9 25.0 all-gather.7
  134.8 52.5 all-gather.3
  271.3 27.9 reduce-scatter.3
  308.9 70.0 reduce-scatter.7
  381.7 49.9 reduce-scatter.5
